TPU v7x, 32 devices: a whole 2x2x4 slice. The times are simulated.
32 devices in a mesh: dp: 8 (over z, x), fsdp: 4 (over y, core).
Axes of the slice: x: 2, y: 2, z: 4, core: 2. Of those that a mesh axis runs over, the one named last changes fastest.
Arguments:
- patches: bfloat16 [8, 4, 192, 64], P('dp', 'fsdp'), may hold values from -6 to 6
- noise: bfloat16 [8, 4, 192, 64], P('dp', 'fsdp'), may hold values from -6 to 6
- bucket: int32 [8, 4], P(None, 'fsdp'), may hold values from 0 to 11
- tstep: int32 [8, 4], P('dp', 'fsdp'), may hold values from 0 to 999
- dest: int32 [8, 4], P(None, 'fsdp'), may hold values from 0 to 7, as said below
- embed_weight: bfloat16 [64, 2432], replicated, may hold values from -0.75 to 0.75
- gain: float32 [2432], replicated, may hold values from 0.1 to 1.9
- proj_weight: bfloat16 [2432, 1216], P('fsdp'), may hold values from -0.125 to 0.125
- cotangent: bfloat16 [8, 4, 2, 192, 1216], P('dp', 'fsdp'), may hold values from -6 to 6
Outputs:
- projected: bfloat16 [8, 4, 2, 192, 1216], P('dp', 'fsdp')
- embed_grad: float32 [64, 2432], replicated
Inputs may be any that keep to these rules, and one draw needn't show every extreme that they name: `dest`: in every column f, each dp index is named by at most 2 images and by exactly 2 for some.
All inputs are finite; a program needn't handle non-finite values.
Results may differ from a plain program's by a relative error of at most 0.006.
Values may be sent and summed in bfloat16 or wider, within the bound.
A program may use at most 64 MiB of HBM per device.

v0:
```python
import jax
import jax.numpy as jnp
from jax import lax
from jax.sharding import PartitionSpec as P

TOK_MAX = 192
CAP = 2
BUCKETS = 12
TSTEPS = 1000


norm_eps = 1e-06


def lengths_of(bucket):
    stride = max(1, TOK_MAX // (2 * BUCKETS))
    return TOK_MAX - bucket * stride


def noise_level(tstep, length):
    frac = (tstep.astype(jnp.float32) + 1.0) / TSTEPS
    shift = 1.0 + 2.0 * length.astype(jnp.float32) / TOK_MAX
    return shift * frac / (1.0 + (shift - 1.0) * frac)


def body(patches, noise, bucket, tstep, dest, embed_weight, gain, proj_weight, cotangent):
    n_dp = lax.axis_size("dp")
    n_fsdp = lax.axis_size("fsdp")
    myself = lax.axis_index("dp")
    feats = patches.shape[-1]
    width = proj_weight.shape[1]
    total_rows = CAP * TOK_MAX
    length_all = lengths_of(bucket[:, 0])
    dest_col = dest[:, 0]
    source_ids = jnp.arange(n_dp, dtype=jnp.int32)
    my_len = jnp.sum(jnp.where(source_ids == myself, length_all, 0))
    level = noise_level(tstep[0, 0], my_len)
    rows = jnp.arange(TOK_MAX, dtype=jnp.int32)
    mixed = (1.0 - level) * patches[0, 0].astype(jnp.float32) + level * noise[0, 0].astype(
        jnp.float32
    )
    latent = jnp.where(rows[:, None] < my_len, mixed, 0.0).astype(jnp.bfloat16)
    same = dest_col[:, None] == dest_col[None, :]
    earlier = source_ids[None, :] < source_ids[:, None]
    slot = jnp.sum((same & earlier).astype(jnp.int32), axis=1)
    slot_ids = jnp.arange(CAP, dtype=jnp.int32)
    chosen = (dest_col[None, :] == myself) & (slot[None, :] == slot_ids[:, None])
    plen = jnp.sum(jnp.where(chosen, length_all[None, :], 0), axis=1)
    arrived = lax.all_gather(latent[None], "dp", axis=0, tiled=True)
    packed = jnp.dot(
        chosen.astype(jnp.bfloat16),
        arrived.reshape(n_dp, TOK_MAX * feats),
        preferred_element_type=jnp.float32,
    )
    packed = packed.astype(jnp.bfloat16).reshape(total_rows, feats)
    hidden = jnp.dot(packed, embed_weight, preferred_element_type=jnp.float32)
    centered_input = hidden - jnp.mean(hidden, axis=1, keepdims=True)
    inverse_deviation = lax.rsqrt(
        jnp.mean(centered_input * centered_input, axis=1, keepdims=True) + norm_eps
    )
    standardized_input = centered_input * inverse_deviation
    normed_rows = (standardized_input * gain).astype(jnp.bfloat16)
    valid = (rows[None, :] < plen[:, None]).reshape(total_rows, 1)
    cot = cotangent[0, 0].reshape(total_rows, width)
    masked = jnp.where(valid, cot, jnp.zeros_like(cot))
    full_weight = lax.all_gather(proj_weight, "fsdp", axis=0, tiled=True)
    output = jnp.dot(normed_rows, full_weight, preferred_element_type=jnp.float32)
    back = lax.dot_general(
        masked, full_weight, (((1,), (1,)), ((), ())), preferred_element_type=jnp.float32
    )
    input_gradient = back * gain
    hidden_gradient = (
        input_gradient
        - jnp.mean(input_gradient, axis=1, keepdims=True)
        - standardized_input * jnp.mean(input_gradient * standardized_input, axis=1, keepdims=True)
    ) * inverse_deviation
    hidden_gradient = hidden_gradient.astype(jnp.bfloat16)
    partial_value = lax.dot_general(
        packed, hidden_gradient, (((0,), (0,)), ((), ())), preferred_element_type=jnp.float32
    )
    total = lax.psum(partial_value, ("dp", "fsdp"))
    embed_grad = total * float(n_dp * n_fsdp * TOK_MAX) ** (-0.5)
    projected = output.astype(jnp.bfloat16).reshape(1, 1, CAP, TOK_MAX, width)
    return (projected, embed_grad)


def solution(mesh):
    placed = (
        P("dp", "fsdp", None, None),
        P("dp", "fsdp", None, None),
        P(None, "fsdp"),
        P("dp", "fsdp"),
        P(None, "fsdp"),
        P(),
        P(),
        P("fsdp", None),
        P("dp", "fsdp", None, None, None),
    )
    return jax.shard_map(
        body,
        mesh=mesh,
        in_specs=placed,
        out_specs=(P("dp", "fsdp", None, None, None), P()),
        check_vma=False,
    )
```

profile of v0, /device:TPU:0, one launch (start us, length us, event | category | flops | bytes accessed | tf_op | source)
XLA Modules:
  0.0 205.2 jit_solution(9802073919326458462)
XLA Ops:
  7.2 0.0 copy-start
  7.2 0.0 all-gather.2.cloned.1.call-start
  7.2 0.7 all-gather.2.cloned.1.call-update
  7.9 0.0 all-reduce.2.cloned.1.call-start
  8.0 1.3 fusion.7
  10.6 0.7 iota_compare_fusion.2
  11.3 0.8 fusion.4
  12.1 32.6 %all_gather.6 = bf16[8,192,64]{1,2,0:T(8,128)(2,1)S(1)} all-gather(bf16[1,192,64]{1,2,0:T(8,128)(2,1)S(1)} %fusion.4), channel_id=1, replica_groups=mesh['dp'=8,'fsdp'=4] {'dp'}, dimensions={0}, use_global_device_ids=true | all-gather | bytes 221184 | tf_op jit(solution)/shard_map/all_gather | solution.py:49
  44.6 0.2 copy.16
  44.9 0.4 reshape.138
  45.2 0.9 convert_reduce_fusion
  46.2 0.7 broadcast_compare_fusion
  46.8 0.2 convolution_convert_fusion
  47.0 0.1 reshape.139
  47.1 0.7 subtract_bitcast_fusion
  47.8 0.1 select_reduce_fusion
  47.9 0.1 iota_compare_fusion.1
  48.0 0.1 lt.52
  48.1 0.7 fusion.10
  48.8 0.0 copy-start.4
  48.9 1.9 copy-done.1
  50.7 0.5 multiply_reduce_fusion.1
  51.2 0.2 bitcast_select_fusion
  51.4 6.9 %all-gather.2.cloned.1.call-done = bf16[2432,1216]{1,0:T(8,128)(2,1)} async-done(((bf16[608,1216]{1,0:T(8,128)(2,1)}), bf16[2432,1216]{1,0:T(8,128)(2,1)}) %all-gather.2.cloned.1.call-update) | async-done | bytes 5914640 | tf_op jit(solution)/shard_map/all_gather | solution.py:66
  58.3 0.0 copy-done.4
  58.3 7.0 %fusion.9 = (f32[384]{0:T(512)S(1)}, f32[384]{0:T(512)S(1)}, f32[384,2432]{1,0:T(8,128)S(1)}) fusion(f32[384]{0:T(512)S(1)} %add_rsqrt_fusion, f32[384,2432]{1,0:T(8,128)} %copy-done.1, f32[384]{0:T(512)S(1)} %broadcast_multiply_fusion.3, f32[2432]{0:T(1024)S(1)} %copy-done.4, bf16[384,1216]{1,0:T(8,128)(2,1)S(1)} %bitcast_select_fusion, ...), kind=kOutput, calls=%fused_computation.33 | convolution fusion | flops 2276817920 | bytes 14335488 | tf_op jit(solution)/shard_map/dot_general | solution.py:68
  65.3 1.9 fusion.3
  67.3 0.0 all-reduce.2.cloned.1.call-update
  67.3 7.4 %convolution_convert_fusion.1 = bf16[384,1216]{0,1:T(8,128)(2,1)S(1)} fusion(bf16[2432,1216]{1,0:T(8,128)(2,1)} %all-gather.2.cloned.1.call-done, f32[384,2432]{1,0:T(8,128)} %copy-done.1, f32[2432]{0:T(1024)S(1)} %copy-done.4, f32[384]{0:T(512)S(1)} %add_rsqrt_fusion, f32[384]{0:T(512)S(1)} %broadcast_multiply_fusion.3), kind=kOutput, calls=%fused_computation.7 | convolution fusion | flops 2275418112 | bytes 10596864 | tf_op jit(solution)/shard_map/dot_general | solution.py:67
  74.7 1.6 copy.17
  76.3 120.1 %all-reduce.2.cloned.1.call-done = f32[64,2432]{1,0:T(8,128)} async-done(((f32[64,2432]{1,0:T(8,128)}), f32[64,2432]{1,0:T(8,128)}) %all-reduce.2.cloned.1.call-update) | async-done | bytes 622608 | tf_op jit(solution)/shard_map/psum | solution.py:81
  196.4 2.0 broadcast_multiply_fusion
  (9 shorter events, 0.0 us)
Async XLA Ops:
  7.2 40.9 %copy-start = (bf16[64,2432]{1,0:T(8,128)(2,1)S(1)}, bf16[64,2432]{1,0:T(8,128)(2,1)}, u32[]{:S(2)}) copy-start(bf16[64,2432]{1,0:T(8,128)(2,1)} %param.14) | copy-start | bytes 933892
  7.2 51.1 %all-gather.2.cloned.1.call-start = ((), (), s32[]{:S(2)}) async-start(), calls=%async_computation | async-start | bytes 7782400 | tf_op jit(solution)/shard_map/all_gather | solution.py:66
  7.9 188.5 %all-reduce.2.cloned.1.call-start = ((), (), s32[]{:S(2)}) async-start(), calls=%async_computation.1 | async-start | bytes 1245184 | tf_op jit(solution)/shard_map/psum | solution.py:81
  48.1 3.1 %copy-start.3 = (bf16[1,1,2,192,1216]{4,3,2,1,0:T(8,128)(2,1)S(1)}, bf16[1,1,2,192,1216]{4,3,2,1,0:T(8,128)(2,1)}, u32[]{:S(2)}) copy-start(bf16[1,1,2,192,1216]{4,3,2,1,0:T(8,128)(2,1)} %param.17) | copy-start | bytes 2801668
  48.8 1.9 copy-start.1
  48.8 9.5 %copy-start.4 = (f32[2432]{0:T(1024)S(1)}, f32[2432]{0:T(1024)}, u32[]{:S(2)}) copy-start(f32[2432]{0:T(1024)} %param.15) | copy-start | bytes 29188
  58.3 7.0 %copy-start.2 = (f32[384,2432]{1,0:T(8,128)S(1)}, f32[384,2432]{1,0:T(8,128)}, u32[]{:S(2)}) copy-start(f32[384,2432]{1,0:T(8,128)} %copy-done.1) | copy-start | bytes 11206660
Sparse Core Ops, SparseCore 0:
  9.5 48.6 all-gather.1
  67.4 128.9 all-reduce.1
where the time goes:
time: 205 us
  waiting for transfers between devices  128 us (62%)
  blocking collectives  32.6 us (16%)
  matrix products  17.3 us (8%)
  between operations  15.5 us (8%)
  other arithmetic  7.85 us (4%)
  local copies, waits for them, and re-layouts  4.31 us (2%)
    psum x1, waiting for transfers between devices, body(): total = lax.psum(partial_value, ('dp', 'fsdp'))  120 us
    all_gather x1, blocking collectives, body(): arrived = lax.all_gather(latent[None], 'dp', axis=0, tiled=True)  32.6 us
    dot_general x1, matrix products, body(): jnp.dot(normed_rows, full_weight, preferred_element_type=jnp.float32)  7.39 us
    dot_general x1, matrix products, body(): lax.dot_general(masked, full_weight, (((1,), (1,)), ((), ())), preferred_...  7.03 us
    all_gather x1, waiting for transfers between devices, body(): full_weight = lax.all_gather(proj_weight, 'fsdp', axis=0, tiled=True)  6.86 us
  transfers between devices with their start and end apart: 2, of which 2 were waited for; matrix products, arithmetic and copies ran while one was open for 8% of the time, Pallas kernels for 0%

commit v1 on v0

v1 whole, which is shorter than its diff:
```python
import functools

import jax
import jax.numpy as jnp
from jax import lax
from jax.experimental import pallas as pl
from jax.experimental.pallas import tpu as pltpu
from jax.sharding import PartitionSpec as P

BUCKETS = 12
TSTEPS = 1000
EPS = 1e-06
F32 = jnp.float32
BF16 = jnp.bfloat16
MESH = pl.DeviceIdType.MESH
NT = (((1,), (1,)), ((), ()))
PIECES = 4


def cut(rows, pieces):
    step = -(-rows // (16 * pieces)) * 16
    return [(a, min(step, rows - a)) for a in range(0, rows, step)]


def kernel(
    n_dp, n_fs, share, owners, quota,
    bucket, tstep, dest, patches, noise, embed, gain, weight, cot,
    out, grad,
    lat, arr, packed, packed_t, masked, full, emb, gains, xhat, normed, gs, acc, obuf, stats,
    st, ra, sb, rb, fd, ff,
    lat_s, lat_r, own_s, own_r, y_s, y_r, x_s, x_r, pa_s, pa_r, pb_s, pb_r,
    a_s, a_r, b_s, b_r, c_s, c_r, d_s, d_r, o_s,
):
    dp, fs = lax.axis_index("dp"), lax.axis_index("fsdp")
    y, c = fs // 2, fs % 2
    n_y = n_fs // 2
    cap, tok, width = cot.shape
    feats = patches.shape[1]
    dim = embed.shape[1]
    depth = weight.shape[0]
    unit = depth // share
    units = n_fs * share
    half = tok // 2
    h = dp % 2 if share == 2 else 0
    mate = dp + 1 - 2 * (dp % 2)
    partner = y * 2 + 1 - c

    def shard(j, core):
        return ((y + j) % n_y) * 2 + core

    def copy(src, dst, send, recv, to):
        return pltpu.make_async_remote_copy(
            src_ref=src, dst_ref=dst, send_sem=send, recv_sem=recv,
            device_id={"dp": to[0], "fsdp": to[1]}, device_id_type=MESH,
        )

    barrier = pltpu.get_barrier_semaphore()
    for k in range(1, n_dp):
        pl.semaphore_signal(
            barrier, inc=1, device_id={"dp": (dp + k) % n_dp, "fsdp": fs}, device_id_type=MESH
        )
    for k in range(1, n_fs):
        pl.semaphore_signal(
            barrier, inc=1, device_id={"dp": dp, "fsdp": (fs + k) % n_fs}, device_id_type=MESH
        )

    stride = max(1, tok // (2 * BUCKETS))
    my_len = tok - stride * bucket[dp, 0]
    frac = (jnp.full((1, feats), tstep[0, 0]).astype(F32) + 1.0) / TSTEPS
    shift = 1.0 + 2.0 * jnp.full((1, feats), my_len).astype(F32) / tok
    level = shift * frac / (1.0 + (shift - 1.0) * frac)
    rows = lax.broadcasted_iota(jnp.int32, (tok, feats), 0)
    mixed = (1.0 - level) * patches[...].astype(F32) + level * noise[...].astype(F32)
    mixed = jnp.where(rows < my_len, mixed, 0.0)
    mine = jnp.concatenate([mixed[:half], mixed[half:]], axis=1).astype(BF16)
    lat[...] = mine
    arr[dp] = mine

    pl.semaphore_wait(barrier, n_dp + n_fs - 2)

    sends = []
    lats = []
    for k in range(1, n_dp):
        cp = copy(lat, arr.at[dp], lat_s.at[k], lat_r.at[k], ((dp + k) % n_dp, fs))
        cp.start()
        lats.append(cp)
    parts = cut(unit, PIECES)
    base = pl.multiple_of(h * unit, 16) if share == 2 else 0
    other = pl.multiple_of((1 - h) * unit, 16) if share == 2 else 0
    ys = {}
    for j in range(1, n_y):
        for p, (at, size) in enumerate(parts):
            sel = pl.ds(pl.multiple_of(base + at, 16), size)
            ys[j, p] = copy(
                weight.at[sel], full.at[fs, sel], y_s.at[j, p], y_r.at[j, p],
                (dp, ((y + n_y - j) % n_y) * 2 + c),
            )
            ys[j, p].start()
    own = copy(weight, full.at[fs], own_s, own_r, (dp, partner))
    own.start()

    count = jnp.int32(0)
    plen = [jnp.int32(0)] * cap
    chosen = []
    for i in range(n_dp):
        hit = (dest[i, 0] == dp).astype(jnp.int32)
        pick = [hit * (count == s).astype(jnp.int32) for s in range(cap)]
        length = tok - stride * bucket[i, 0]
        plen = [a + b * length for a, b in zip(plen, pick)]
        chosen.append(pick)
        count = count + hit
    cot_rows = lax.broadcasted_iota(jnp.int32, (tok, width), 0)
    for s in range(cap):
        masked[s * tok : (s + 1) * tok] = jnp.where(
            cot_rows < plen[s], cot[s].astype(F32), 0.0
        ).astype(BF16)
    for u in range(units):
        emb[u] = embed[:, u * unit : (u + 1) * unit]
        gains[u] = gain[:, u * unit : (u + 1) * unit]

    def block(w_ref, row):
        return w_ref[pl.ds(pl.multiple_of(row, 8), unit), :]

    def back(u, w):
        got = lax.dot_general(masked[...], w, NT, preferred_element_type=F32)
        gs[u] = got * gains[u]

    def sums(u):
        g = gs[u]
        stats[2] += jnp.sum(g, axis=1, keepdims=True)
        stats[3] += jnp.sum(g * xhat[u], axis=1, keepdims=True)

    def project(u, w):
        acc[...] += jnp.dot(normed[u], w, preferred_element_type=F32)

    @pl.loop(0, share)
    def _(i):
        back(fs * share + i, block(weight, i * unit))

    acc[...] = jnp.zeros_like(acc)
    stats[...] = jnp.zeros_like(stats)

    for cp in lats:
        cp.wait_recv()
    for s in range(cap):
        total = jnp.zeros((half, 2 * feats), F32)
        for i in range(n_dp):
            total += jnp.where(chosen[i][s] > 0, arr[i].astype(F32), 0.0)
        packed[s * tok : s * tok + half] = total[:, :feats].astype(BF16)
        packed[s * tok + half : (s + 1) * tok] = total[:, feats:].astype(BF16)
    packed_t[...] = packed[...].astype(F32).T.astype(BF16)

    @pl.loop(0, units)
    def _(u):
        hid = jnp.dot(packed[...], emb[u], preferred_element_type=F32)
        xhat[u] = hid
        stats[0] += jnp.sum(hid, axis=1, keepdims=True)

    mean = stats[0] * (1.0 / dim)

    @pl.loop(0, units)
    def _(u):
        cen = xhat[u] - mean
        xhat[u] = cen
        stats[1] += jnp.sum(cen * cen, axis=1, keepdims=True)

    rstd = lax.rsqrt(stats[1] * (1.0 / dim) + EPS)

    @pl.loop(0, units)
    def _(u):
        std = xhat[u] * rstd
        xhat[u] = std
        normed[u] = (std * gains[u]).astype(BF16)

    relayed = {}

    def relay_y(j, p):
        at, size = parts[p]
        ys[j, p].wait_recv()
        sel = pl.ds(pl.multiple_of(base + at, 16), size)
        src = full.at[shard(j, c), sel]
        if share == 2:
            cp = copy(src, src, x_s.at[j, p], x_r.at[j, p], (mate, fs))
            cp.start()
            relayed["x", j, p] = cp
        cp = copy(src, src, pa_s.at[j, p], pa_r.at[j, p], (dp, partner))
        cp.start()
        relayed["pa", j, p] = cp

    def relay_x(j, p):
        at, size = parts[p]
        relayed["x", j, p].wait_recv()
        sel = pl.ds(pl.multiple_of(other + at, 16), size)
        src = full.at[shard(j, c), sel]
        cp = copy(src, src, pb_s.at[j, p], pb_r.at[j, p], (dp, partner))
        cp.start()
        relayed["pb", j, p] = cp

    last = len(parts)
    firsts = [(1, p) for p in range(last)] if n_y > 1 else []
    for key in firsts[:1]:
        relay_y(*key)

    @pl.loop(0, share)
    def _(i):
        u = fs * share + i
        sums(u)
        project(u, block(weight, i * unit))

    for key in firsts[1:2]:
        relay_y(*key)
    own.wait_recv()

    def work(s, part):
        u = s * share + part
        w = block(full.at[s], part * unit)
        back(u, w)
        sums(u)
        project(u, w)

    @pl.loop(0, share)
    def _(i):
        work(partner, i)

    for j in range(1, n_y):
        for p in range(last):
            if ("pa", j, p) not in relayed:
                relay_y(j, p)
        work(shard(j, c), h)
        if share == 2:
            for p in range(last // 2):
                relay_x(j, p)
        for p in range(last):
            relayed["pa", j, p].wait_recv()
        work(shard(j, 1 - c), h)
        if share == 2:
            for p in range(last // 2, last):
                relay_x(j, p)
            work(shard(j, c), 1 - h)
            for p in range(last):
                relayed["pb", j, p].wait_recv()
            work(shard(j, 1 - c), 1 - h)

    mean_g = stats[2] * (1.0 / dim)
    mean_gx = stats[3] * (1.0 / dim)
    span = share * feats

    @pl.loop(0, n_fs)
    def _(s):
        for i in range(share):
            u = s * share + i
            dh = ((gs[u] - mean_g - xhat[u] * mean_gx) * rstd).astype(BF16)
            st[s, i * feats : (i + 1) * feats] = jnp.dot(
                packed_t[...], dh, preferred_element_type=F32
            ).astype(BF16)

    phase = []
    for k in range(1, n_fs):
        to = (fs + k) % n_fs
        cp = copy(st.at[to], ra.at[k], a_s.at[k], a_r.at[k], (dp, to))
        cp.start()
        phase.append(cp)

    obuf[...] = acc[...].astype(BF16)
    write = pltpu.make_async_copy(obuf, out, o_s)
    write.start()

    total = st[fs].astype(F32)
    for k, cp in enumerate(phase):
        cp.wait_recv()
        total += ra[k + 1].astype(F32)
    sb[...] = total.astype(BF16)
    sends += phase

    everyone = owners == n_dp

    def guard(cond, action):
        if everyone:
            action()
        else:
            pl.when(cond)(action)

    def piece(d):
        return pl.ds(pl.multiple_of(d * quota, 16), quota)

    owner = dp < owners
    scatter, spread = {}, {}
    for k in range(1, n_dp):
        to = (dp + k) % n_dp
        safe = to if everyone else to % owners
        scatter[k] = copy(sb.at[piece(safe)], rb.at[k], b_s.at[k], b_r.at[k], (to, fs))
        guard(to < owners, scatter[k].start)

    here = piece(dp if everyone else dp % owners)

    def reduce():
        mine = sb[here].astype(F32)
        for k in range(1, n_dp):
            scatter[k].wait_recv()
            mine += rb[k].astype(F32)
        fd[here] = mine.astype(BF16)

    guard(owner, reduce)
    for k in range(1, n_dp):
        to = (dp + k) % n_dp
        spread[k] = copy(fd.at[here], fd.at[here], c_s.at[k], c_r.at[k], (to, fs))
        guard(owner, spread[k].start)
    for k in range(1, n_dp):
        source = (dp + n_dp - k) % n_dp
        guard(source < owners, spread[k].wait_recv)

    phase = []
    for k in range(1, n_fs):
        to = (fs + k) % n_fs
        cp = copy(fd, ff.at[fs], d_s.at[k], d_r.at[k], (dp, to))
        cp.start()
        phase.append(cp)
    ff[fs] = fd[...]
    for cp in phase:
        cp.wait_recv()
    sends += phase
    scale = float(n_dp * n_fs * tok) ** (-0.5)
    for u in range(units):
        s, i = u // share, u % share
        grad[:, u * unit : (u + 1) * unit] = (
            ff[s, i * feats : (i + 1) * feats].astype(F32) * scale
        )

    write.wait()
    for cp in lats + [own] + list(ys.values()) + list(relayed.values()) + sends:
        cp.wait_send()
    for k in range(1, n_dp):
        to = (dp + k) % n_dp
        guard(to < owners, scatter[k].wait_send)
        guard(owner, spread[k].wait_send)


def body(patches, noise, bucket, tstep, dest, embed_weight, gain, proj_weight, cotangent):
    n_dp = lax.axis_size("dp")
    n_fs = lax.axis_size("fsdp")
    tok, feats = patches.shape[2:]
    depth, width = proj_weight.shape
    dim = gain.shape[0]
    cap = cotangent.shape[2]
    share = 2 if n_dp % 2 == 0 and depth % 32 == 0 else 1
    unit = depth // share
    units = n_fs * share
    rows = cap * tok
    span = share * feats
    quota = -(-span // (16 * n_dp)) * 16
    owners = span // quota
    n_y = n_fs // 2
    pieces = len(cut(unit, PIECES))
    vmem = pl.BlockSpec(memory_space=pltpu.VMEM)
    smem = pl.BlockSpec(memory_space=pltpu.SMEM)
    dma = pltpu.SemaphoreType.DMA
    link = dma((n_y, pieces))
    projected, grad = pl.pallas_call(
        functools.partial(kernel, n_dp, n_fs, share, owners, quota),
        out_shape=(
            jax.ShapeDtypeStruct((rows, width), BF16),
            jax.ShapeDtypeStruct((feats, dim), F32),
        ),
        in_specs=[smem] * 3 + [vmem] * 6,
        out_specs=(pl.BlockSpec(memory_space=pl.ANY), vmem),
        scratch_shapes=[
            pltpu.VMEM((tok // 2, 2 * feats), BF16),
            pltpu.VMEM((n_dp, tok // 2, 2 * feats), BF16),
            pltpu.VMEM((rows, feats), BF16),
            pltpu.VMEM((feats, rows), BF16),
            pltpu.VMEM((rows, width), BF16),
            pltpu.VMEM((n_fs, depth, width), BF16),
            pltpu.VMEM((units, feats, unit), BF16),
            pltpu.VMEM((units, 1, unit), F32),
            pltpu.VMEM((units, rows, unit), F32),
            pltpu.VMEM((units, rows, unit), BF16),
            pltpu.VMEM((units, rows, unit), F32),
            pltpu.VMEM((rows, width), F32),
            pltpu.VMEM((rows, width), BF16),
            pltpu.VMEM((4, rows, 1), F32),
            pltpu.VMEM((n_fs, span, unit), BF16),
            pltpu.VMEM((n_fs, span, unit), BF16),
            pltpu.VMEM((span, unit), BF16),
            pltpu.VMEM((n_dp, quota, unit), BF16),
            pltpu.VMEM((span, unit), BF16),
            pltpu.VMEM((n_fs, span, unit), BF16),
            dma((n_dp,)), dma((n_dp,)), dma, dma,
            link, link, link, link, link, link, link, link,
            dma((n_fs,)), dma((n_fs,)), dma((n_dp,)), dma((n_dp,)),
            dma((n_dp,)), dma((n_dp,)), dma((n_fs,)), dma((n_fs,)), dma,
        ],
        compiler_params=pltpu.CompilerParams(
            collective_id=0, has_side_effects=True, vmem_limit_bytes=62 * 1024 * 1024
        ),
    )(
        bucket, tstep, dest, patches[0, 0], noise[0, 0], embed_weight, gain[None],
        proj_weight, cotangent[0, 0],
    )
    return projected.reshape(1, 1, cap, tok, width), grad


def solution(mesh):
    placed = (
        P("dp", "fsdp", None, None),
        P("dp", "fsdp", None, None),
        P(None, "fsdp"),
        P("dp", "fsdp"),
        P(None, "fsdp"),
        P(),
        P(),
        P("fsdp", None),
        P("dp", "fsdp", None, None, None),
    )
    return jax.shard_map(
        body,
        mesh=mesh,
        in_specs=placed,
        out_specs=(P("dp", "fsdp", None, None, None), P()),
        check_vma=False,
    )
```

time: 205 us -> 74.1 us (0.36)
  waiting for transfers between devices: 128 us -> 0 us
  Pallas kernels: 0 us -> 62.4 us
  blocking collectives: 32.6 us -> 0 us
  matrix products: 17.3 us -> 0 us
  between operations: 15.5 us -> 1.3 us
  other arithmetic: 7.85 us -> 0 us
  local copies, waits for them, and re-layouts: 4.31 us -> 10 us
    psum x1 -> x0, waiting for transfers between devices: 120 us -> none  [body(): total = lax.psum(partial_value, ('dp', 'fsdp'))]
    pallas_call x0 -> x1, Pallas kernels: none -> 62.4 us  [body(): pl.pallas_call(functools.partial(kernel, n_dp, n_fs, share, owners, quota...]
    all_gather x1 -> x0, blocking collectives: 32.6 us -> none  [body(): arrived = lax.all_gather(latent[None], 'dp', axis=0, tiled=True)]
    dot_general x5 -> x0, matrix products: 17.3 us -> none  [the longest x1 7.39 us: body(): jnp.dot(normed_rows, full_weight, preferred_element_type=jnp.float32)]
    all_gather x1 -> x0, waiting for transfers between devices: 6.86 us -> none  [body(): full_weight = lax.all_gather(proj_weight, 'fsdp', axis=0, tiled=True)]
    unnamed x10 -> x8, local copies, waits for them, and re-layouts: 1.88 us -> 8.7 us
    reduce_sum x4 -> x0, other arithmetic: 2.84 us -> none  [the longest x1 1.3 us: body(): my_len = jnp.sum(jnp.where(source_ids == myself, length_all, 0))]
  transfers between devices with their start and end apart: 2 -> 0, of which waited for: 2 -> 0; matrix products, arithmetic and copies ran while one was open for 8% -> 0% of each run, Pallas kernels for 0% -> 0%
where the time goes in v1:
time: 74.1 us; the launch traced here: 73.7 us
  Pallas kernels  62.4 us (84%)
  local copies, waits for them, and re-layouts  10 us (13%)
  between operations  1.3 us (2%)
    pallas_call x1, Pallas kernels, body(): pl.pallas_call(functools.partial(kernel, n_dp, n_fs, share, owners, quota...  62.4 us
    unnamed x8, local copies, waits for them, and re-layouts  8.7 us

profile of v1, /device:TPU:0, one launch (start us, length us, event | category | flops | bytes accessed | tf_op | source)
XLA Modules:
  0.0 73.7 jit_solution(10904310055917156487)
XLA Ops:
  1.3 1.3 %copy.13.bucket = s32[8,1]{1,0:T(8,128)} copy(s32[8,1]{0,1:T(1,128)} %param.11) | data formatting | bytes 64 | tf_op args[2]
  2.6 1.3 %copy.14.dest = s32[8,1]{1,0:T(8,128)} copy(s32[8,1]{0,1:T(1,128)} %param.13) | data formatting | bytes 64 | tf_op args[4]
  3.9 1.3 %broadcast_in_dim.3.gain = f32[1,2432]{1,0:T(1,128)} reshape(f32[2432]{0:T(1024)} %param.15) | data formatting | bytes 19456 | tf_op jit(solution)/shard_map/broadcast_in_dim | solution.py:396
  5.2 1.5 %copy.11 = bf16[1,1,192,64]{3,2,1,0:T(8,128)(2,1)} copy(bf16[1,1,192,64]{2,3,1,0:T(8,128)(2,1)} %param.9) | data formatting | bytes 49152 | tf_op args[0]
  6.7 1.5 %copy.12 = bf16[1,1,192,64]{3,2,1,0:T(8,128)(2,1)} copy(bf16[1,1,192,64]{2,3,1,0:T(8,128)(2,1)} %param.10) | data formatting | bytes 49152 | tf_op args[1]
  8.2 62.4 %shard_map.104 = (bf16[384,1216]{1,0:T(8,128)(2,1)}, f32[64,2432]{1,0:T(8,128)}) custom-call(s32[8,1]{1,0:T(8,128)} %copy.13.bucket, s32[1,1]{1,0:T(1,128)S(6)} %copy.17.tstep, s32[8,1]{1,0:T(8,128)} %copy.14.dest, bf16[192,64]{1,0:T(8,128)(2,1)} %bitcast.6, bf16[192,64]{1,0:T(8,128)(2,1)} %bitcast.7, bf16[64,2432]{1,0:T(8,128)(2,1)} %embed.1, ...), custom_call_target="tpu_custom_call" | custom-call | tf_op jit(solution)/shard_map/pallas_call | solution.py:358
  70.6 0.0 copy-start
  70.6 2.3 %copy.18 = bf16[1,1,2,192,1216]{4,3,2,1,0:T(8,128)(2,1)} copy(bf16[1,1,2,192,1216]{4,3,2,1,0:T(8,128)(2,1)} %bitcast.5) | data formatting | bytes 1867776
  72.9 0.0 copy-done
  72.9 0.8 %copy.19 = f32[64,2432]{1,0:T(8,128)} copy(f32[64,2432]{1,0:T(8,128)S(1)} %copy-done) | data formatting | bytes 1245184
Async XLA Ops:
  70.6 2.3 %copy-start = (f32[64,2432]{1,0:T(8,128)S(1)}, f32[64,2432]{1,0:T(8,128)}, u32[]{:S(2)}) copy-start(f32[64,2432]{1,0:T(8,128)} %get-tuple-element.9) | copy-start | bytes 1867780

commit v2 on v1

--- a/solution.py
+++ b/solution.py
@@ -26,16 +26,16 @@
     n_dp, n_fs, share, owners, quota,
     bucket, tstep, dest, patches, noise, embed, gain, weight, cot,
     out, grad,
-    lat, arr, packed, packed_t, masked, full, emb, gains, xhat, normed, gs, acc, obuf, stats,
+    lat, arr, packed, packed_t, masked, full, emb, gains, xhat, normed, gs, acc, stats,
     st, ra, sb, rb, fd, ff,
     lat_s, lat_r, own_s, own_r, y_s, y_r, x_s, x_r, pa_s, pa_r, pb_s, pb_r,
-    a_s, a_r, b_s, b_r, c_s, c_r, d_s, d_r, o_s,
+    a_s, a_r, b_s, b_r, c_s, c_r, d_s, d_r,
 ):
     dp, fs = lax.axis_index("dp"), lax.axis_index("fsdp")
     y, c = fs // 2, fs % 2
     n_y = n_fs // 2
     cap, tok, width = cot.shape
-    feats = patches.shape[1]
+    feats = patches.shape[0]
     dim = embed.shape[1]
     depth = weight.shape[0]
     unit = depth // share
@@ -65,13 +65,13 @@
         )
 
     stride = max(1, tok // (2 * BUCKETS))
-    my_len = tok - stride * bucket[dp, 0]
-    frac = (jnp.full((1, feats), tstep[0, 0]).astype(F32) + 1.0) / TSTEPS
-    shift = 1.0 + 2.0 * jnp.full((1, feats), my_len).astype(F32) / tok
+    my_len = tok - stride * bucket[0, dp]
+    frac = (jnp.full((1, tok), tstep[0, 0]).astype(F32) + 1.0) / TSTEPS
+    shift = 1.0 + 2.0 * jnp.full((1, tok), my_len).astype(F32) / tok
     level = shift * frac / (1.0 + (shift - 1.0) * frac)
-    rows = lax.broadcasted_iota(jnp.int32, (tok, feats), 0)
+    rows = lax.broadcasted_iota(jnp.int32, (feats, tok), 1)
     mixed = (1.0 - level) * patches[...].astype(F32) + level * noise[...].astype(F32)
-    mixed = jnp.where(rows < my_len, mixed, 0.0)
+    mixed = jnp.where(rows < my_len, mixed, 0.0).T
     mine = jnp.concatenate([mixed[:half], mixed[half:]], axis=1).astype(BF16)
     lat[...] = mine
     arr[dp] = mine
@@ -103,9 +103,9 @@
     plen = [jnp.int32(0)] * cap
     chosen = []
     for i in range(n_dp):
-        hit = (dest[i, 0] == dp).astype(jnp.int32)
+        hit = (dest[0, i] == dp).astype(jnp.int32)
         pick = [hit * (count == s).astype(jnp.int32) for s in range(cap)]
-        length = tok - stride * bucket[i, 0]
+        length = tok - stride * bucket[0, i]
         plen = [a + b * length for a, b in zip(plen, pick)]
         chosen.append(pick)
         count = count + hit
@@ -114,9 +114,10 @@
         masked[s * tok : (s + 1) * tok] = jnp.where(
             cot_rows < plen[s], cot[s].astype(F32), 0.0
         ).astype(BF16)
+    line = jnp.concatenate([gain[t : t + 1] for t in range(gain.shape[0])], axis=1)
     for u in range(units):
         emb[u] = embed[:, u * unit : (u + 1) * unit]
-        gains[u] = gain[:, u * unit : (u + 1) * unit]
+        gains[u] = line[:, u * unit : (u + 1) * unit]
 
     def block(w_ref, row):
         return w_ref[pl.ds(pl.multiple_of(row, 8), unit), :]
@@ -245,8 +246,7 @@
     mean_gx = stats[3] * (1.0 / dim)
     span = share * feats
 
-    @pl.loop(0, n_fs)
-    def _(s):
+    def term(s):
         for i in range(share):
             u = s * share + i
             dh = ((gs[u] - mean_g - xhat[u] * mean_gx) * rstd).astype(BF16)
@@ -257,13 +257,13 @@
     phase = []
     for k in range(1, n_fs):
         to = (fs + k) % n_fs
+        term(to)
         cp = copy(st.at[to], ra.at[k], a_s.at[k], a_r.at[k], (dp, to))
         cp.start()
         phase.append(cp)
 
-    obuf[...] = acc[...].astype(BF16)
-    write = pltpu.make_async_copy(obuf, out, o_s)
-    write.start()
+    term(fs)
+    out[...] = acc[...].astype(BF16)
 
     total = st[fs].astype(F32)
     for k, cp in enumerate(phase):
@@ -326,7 +326,6 @@
             ff[s, i * feats : (i + 1) * feats].astype(F32) * scale
         )
 
-    write.wait()
     for cp in lats + [own] + list(ys.values()) + list(relayed.values()) + sends:
         cp.wait_send()
     for k in range(1, n_dp):
@@ -358,11 +357,11 @@
     projected, grad = pl.pallas_call(
         functools.partial(kernel, n_dp, n_fs, share, owners, quota),
         out_shape=(
-            jax.ShapeDtypeStruct((rows, width), BF16),
-            jax.ShapeDtypeStruct((feats, dim), F32),
+            pltpu.VMEM((rows, width), BF16),
+            pltpu.VMEM((feats, dim), F32),
         ),
         in_specs=[smem] * 3 + [vmem] * 6,
-        out_specs=(pl.BlockSpec(memory_space=pl.ANY), vmem),
+        out_specs=(vmem, vmem),
         scratch_shapes=[
             pltpu.VMEM((tok // 2, 2 * feats), BF16),
             pltpu.VMEM((n_dp, tok // 2, 2 * feats), BF16),
@@ -376,7 +375,6 @@
             pltpu.VMEM((units, rows, unit), BF16),
             pltpu.VMEM((units, rows, unit), F32),
             pltpu.VMEM((rows, width), F32),
-            pltpu.VMEM((rows, width), BF16),
             pltpu.VMEM((4, rows, 1), F32),
             pltpu.VMEM((n_fs, span, unit), BF16),
             pltpu.VMEM((n_fs, span, unit), BF16),
@@ -387,13 +385,14 @@
             dma((n_dp,)), dma((n_dp,)), dma, dma,
             link, link, link, link, link, link, link, link,
             dma((n_fs,)), dma((n_fs,)), dma((n_dp,)), dma((n_dp,)),
-            dma((n_dp,)), dma((n_dp,)), dma((n_fs,)), dma((n_fs,)), dma,
+            dma((n_dp,)), dma((n_dp,)), dma((n_fs,)), dma((n_fs,)),
         ],
         compiler_params=pltpu.CompilerParams(
-            collective_id=0, has_side_effects=True, vmem_limit_bytes=62 * 1024 * 1024
+            collective_id=0, has_side_effects=True, vmem_limit_bytes=44 * 1024 * 1024
         ),
     )(
-        bucket, tstep, dest, patches[0, 0], noise[0, 0], embed_weight, gain[None],
+        bucket.T, tstep, dest.T, patches[0, 0].T, noise[0, 0].T, embed_weight,
+        gain.reshape(-1, 128),
         proj_weight, cotangent[0, 0],
     )
     return projected.reshape(1, 1, cap, tok, width), grad

time: 74.1 us -> 69.5 us (0.938)
  Pallas kernels: 62.4 us -> 58.9 us
  local copies, waits for them, and re-layouts: 10 us -> 8.87 us
    pallas_call x1, Pallas kernels: 62.4 us -> 58.9 us  [body(): pl.pallas_call(functools.partial(kernel, n_dp, n_fs, share, owners, quota...]
    broadcast_in_dim x1 -> x0, local copies, waits for them, and re-layouts: 1.31 us -> none  [body(): gain[None]]
    unnamed x8 -> x18, local copies, waits for them, and re-layouts: 8.7 us -> 8.87 us
where the time goes in v2:
time: 69.5 us; the launch traced here: 69 us
  Pallas kernels  58.9 us (85%)
  local copies, waits for them, and re-layouts  8.87 us (13%)
  between operations  1.3 us (2%)
    pallas_call x1, Pallas kernels, body(): pl.pallas_call(functools.partial(kernel, n_dp, n_fs, share, owners, quota...  58.9 us
    unnamed x18, local copies, waits for them, and re-layouts  8.87 us

profile of v2, /device:TPU:0, one launch (start us, length us, event | category | flops | bytes accessed | tf_op | source)
XLA Modules:
  0.0 69.0 jit_solution(3414064296307159069)
XLA Ops:
  1.3 0.0 copy-start
  1.3 1.4 %copy-done = bf16[608,1216]{1,0:T(8,128)(2,1)S(1)} copy-done((bf16[608,1216]{1,0:T(8,128)(2,1)S(1)}, bf16[608,1216]{1,0:T(8,128)(2,1)}, u32[]{:S(2)}) %copy-start) | copy-done | bytes 1478680
  2.7 0.0 copy-start.1
  2.7 1.2 %copy-done.1 = bf16[1,1,2,192,1216]{4,3,2,1,0:T(8,128)(2,1)S(1)} copy-done((bf16[1,1,2,192,1216]{4,3,2,1,0:T(8,128)(2,1)S(1)}, bf16[1,1,2,192,1216]{4,3,2,1,0:T(8,128)(2,1)}, u32[]{:S(2)}) %copy-start.1) | copy-done | bytes 933912
  3.9 0.0 copy-start.2
  3.9 1.0 %copy-done.2 = bf16[64,2432]{1,0:T(8,128)(2,1)S(1)} copy-done((bf16[64,2432]{1,0:T(8,128)(2,1)S(1)}, bf16[64,2432]{1,0:T(8,128)(2,1)}, u32[]{:S(2)}) %copy-start.2) | copy-done | bytes 311320
  4.9 0.0 copy-start.3
  4.9 0.8 %copy-done.3 = bf16[1,1,192,64]{2,3,1,0:T(8,128)(2,1)S(1)} copy-done((bf16[1,1,192,64]{2,3,1,0:T(8,128)(2,1)S(1)}, bf16[1,1,192,64]{2,3,1,0:T(8,128)(2,1)}, u32[]{:S(2)}) %copy-start.3) | copy-done | bytes 24600
  5.6 0.0 copy-start.4
  5.6 0.8 %copy-done.4 = bf16[1,1,192,64]{2,3,1,0:T(8,128)(2,1)S(1)} copy-done((bf16[1,1,192,64]{2,3,1,0:T(8,128)(2,1)S(1)}, bf16[1,1,192,64]{2,3,1,0:T(8,128)(2,1)}, u32[]{:S(2)}) %copy-start.4) | copy-done | bytes 24600
  6.4 0.0 copy-start.5
  6.4 0.7 %copy-done.5 = f32[2432]{0:T(1024)S(1)} copy-done((f32[2432]{0:T(1024)S(1)}, f32[2432]{0:T(1024)}, u32[]{:S(2)}) %copy-start.5) | copy-done | bytes 9752
  7.1 0.0 copy-start.6
  7.1 0.7 copy-done.6
  7.7 0.0 copy-start.7
  7.7 0.7 copy-done.7
  8.4 58.9 %shard_map.104 = (bf16[384,1216]{1,0:T(8,128)(2,1)S(1)}, f32[64,2432]{1,0:T(8,128)S(1)}) custom-call(s32[1,8]{1,0:T(1,128)S(1)} %bitcast.16, s32[1,1]{1,0:T(1,128)S(6)} %copy.15.tstep, s32[1,8]{1,0:T(1,128)S(1)} %bitcast.17, bf16[64,192]{1,0:T(8,128)(2,1)S(1)} %bitcast.13, bf16[64,192]{1,0:T(8,128)(2,1)S(1)} %bitcast.14, bf16[64,2432]{1,0:T(8,128)(2,1)S(1)} %copy-done.2, ...), custom_call_target="tpu_custom_call" | custom-call | tf_op jit(solution)/shard_map/pallas_call | solution.py:357
  67.3 0.9 %copy.13 = bf16[1,1,2,192,1216]{4,3,2,1,0:T(8,128)(2,1)} copy(bf16[1,1,2,192,1216]{4,3,2,1,0:T(8,128)(2,1)S(1)} %bitcast.11) | data formatting | bytes 1867776
  68.2 0.8 %copy.14 = f32[64,2432]{1,0:T(8,128)} copy(f32[64,2432]{1,0:T(8,128)S(1)} %get-tuple-element.7) | data formatting | bytes 1245184
Async XLA Ops:
  1.3 1.4 %copy-start = (bf16[608,1216]{1,0:T(8,128)(2,1)S(1)}, bf16[608,1216]{1,0:T(8,128)(2,1)}, u32[]{:S(2)}) copy-start(bf16[608,1216]{1,0:T(8,128)(2,1)} %weight.1) | copy-start | bytes 4435972
  2.7 1.2 %copy-start.1 = (bf16[1,1,2,192,1216]{4,3,2,1,0:T(8,128)(2,1)S(1)}, bf16[1,1,2,192,1216]{4,3,2,1,0:T(8,128)(2,1)}, u32[]{:S(2)}) copy-start(bf16[1,1,2,192,1216]{4,3,2,1,0:T(8,128)(2,1)} %param.17) | copy-start | bytes 2801668
  3.9 1.0 %copy-start.2 = (bf16[64,2432]{1,0:T(8,128)(2,1)S(1)}, bf16[64,2432]{1,0:T(8,128)(2,1)}, u32[]{:S(2)}) copy-start(bf16[64,2432]{1,0:T(8,128)(2,1)} %embed.1) | copy-start | bytes 933892
  4.9 0.8 %copy-start.3 = (bf16[1,1,192,64]{2,3,1,0:T(8,128)(2,1)S(1)}, bf16[1,1,192,64]{2,3,1,0:T(8,128)(2,1)}, u32[]{:S(2)}) copy-start(bf16[1,1,192,64]{2,3,1,0:T(8,128)(2,1)} %param.9) | copy-start | bytes 73732
  5.6 0.8 %copy-start.4 = (bf16[1,1,192,64]{2,3,1,0:T(8,128)(2,1)S(1)}, bf16[1,1,192,64]{2,3,1,0:T(8,128)(2,1)}, u32[]{:S(2)}) copy-start(bf16[1,1,192,64]{2,3,1,0:T(8,128)(2,1)} %param.10) | copy-start | bytes 73732
  6.4 0.7 %copy-start.5 = (f32[2432]{0:T(1024)S(1)}, f32[2432]{0:T(1024)}, u32[]{:S(2)}) copy-start(f32[2432]{0:T(1024)} %param.15) | copy-start | bytes 29188
  7.1 0.7 copy-start.6
  7.7 0.7 copy-start.7
